TPU v7x, 32 devices: a whole 2x2x4 slice. The times are simulated.
32 devices in a mesh: ba: 8 (over z, y), dev: 4 (over x, core).
Axes of the slice: x: 2, y: 2, z: 4, core: 2. Of those that a mesh axis runs over, the one named last changes fastest.
Arguments:
- factors: bfloat16 [16, 512, 1024], P('ba', 'dev'), may hold values from -0.1875 to 0.1875
- amplitudes: bfloat16 [64, 512, 512], P(None, 'dev'), may hold values from -0.375 to 0.375
- pair_order: int32 [64], replicated, may hold values from 0 to 63, each once
- occ_bin: int32 [8], replicated, may hold values from 0 to 127
- vir_bin: int32 [16], replicated, may hold values from 0 to 127
- levels: float32 [128], replicated, may hold values from 0.1 to 0.8
Outputs:
- update: float32 [16, 1024], P('ba', 'dev')
Inputs may be any that keep to these rules, and one draw needn't show every extreme that they name: `pair_order`: each value appears once; entry k names the ordered occupied pair (value // 8, value % 8). `occ_bin`: orbital i has energy minus levels at its bin. `vir_bin`: window virtual a has energy levels at its bin.
All inputs are finite; a program needn't handle non-finite values.
Results may differ from a plain program's by a relative error of at most 0.0029.
Values may be sent and summed in bfloat16 or wider, within the bound.
A program may use at most 64 MiB of HBM per device.

v0:
```python
import jax
import jax.numpy as jnp
from jax import lax
from jax.sharding import PartitionSpec as P

NOCC = 8


level_shift = 0.3


def integral_block(left_side, right_side, contracts):
    left_count, cblock, fitting = left_side.shape
    flat_left = left_side.reshape(left_count * cblock, fitting)
    flat_amps = contracts.reshape(contracts.shape[0], -1)
    results = []
    for position in range(right_side.shape[0]):
        integrals = lax.dot_general(
            flat_left,
            right_side[position],
            (((1,), (1,)), ((), ())),
            preferred_element_type=jnp.float32,
        )
        integrals = integrals.astype(jnp.bfloat16).reshape(left_count, -1)
        results.append(
            lax.dot_general(
                integrals, flat_amps, (((1,), (1,)), ((), ())), preferred_element_type=jnp.float32
            )
        )
    return jnp.stack(results)


def lookup(indices, table):
    choices_range = jnp.arange(table.shape[0], dtype=jnp.int32)
    return jnp.sum(
        jnp.where(indices[:, None] == choices_range[None, :], table[None, :], 0.0), axis=1
    )


def per_device(factors, amplitudes, pair_order, occ_bin, vir_bin, levels):
    owned = factors.shape[0]
    window = owned * lax.axis_size("ba")
    pair_count = amplitudes.shape[0]
    split_rows = window // lax.axis_size("dev")
    swapped = pair_order % NOCC * NOCC + pair_order // NOCC
    matches = swapped[:, None] == pair_order[None, :]
    left_side = lax.all_gather(factors, "ba", axis=0, tiled=True)
    ladder = integral_block(
        left_side, lax.all_gather(factors, "dev", axis=1, tiled=True), amplitudes
    )
    moved = lax.all_to_all(ladder, "ba", split_axis=1, concat_axis=0, tiled=True)
    flipped = jnp.transpose(moved, (1, 0, 2))
    permuter = matches.astype(jnp.float32)
    combined = ladder + jnp.matmul(flipped, permuter.T, precision=lax.Precision.HIGHEST)
    summed = lax.psum_scatter(combined, "dev", scatter_dimension=1, tiled=True)
    virtual_energy = lookup(vir_bin, levels)
    occupied_energy = -lookup(occ_bin, levels)
    pair_energy = lookup(pair_order // NOCC, occupied_energy) + lookup(
        pair_order % NOCC, occupied_energy
    )
    left_energy = lax.dynamic_slice_in_dim(
        virtual_energy, lax.axis_index("dev") * split_rows, split_rows
    )
    right_energy = lax.dynamic_slice_in_dim(virtual_energy, lax.axis_index("ba") * owned, owned)
    denominator = (
        right_energy[:, None, None]
        + left_energy[None, :, None]
        - pair_energy[None, None, :]
        + level_shift
    )
    return (summed / denominator).reshape(owned, split_rows * pair_count)


def solution(mesh):
    return jax.shard_map(
        per_device,
        mesh=mesh,
        in_specs=(P("ba", "dev", None), P(None, "dev", None), P(), P(), P(), P()),
        out_specs=P("ba", "dev"),
        check_vma=False,
    )
```

profile of v0, /device:TPU:0, one launch (start us, length us, event | category | flops | bytes accessed | tf_op | source)
XLA Modules:
  0.0 168.6 jit_solution(17841638818002200709)
XLA Ops:
  6.5 0.0 all-gather.5.cloned.1.call-start
  6.5 0.7 all-gather.5.cloned.1.call-update
  7.3 0.0 all-gather.3.cloned.1.call-start
  7.3 0.7 all-gather.3.cloned.1.call-update
  8.0 0.9 select_reduce_fusion
  8.9 0.1 dynamic_slice.7
  8.9 0.1 dynamic_slice.6
  9.0 0.9 select_reduce_fusion.3
  9.9 0.0 copy-start
  9.9 11.8 %copy.14 = bf16[8,8,128,512]{3,1,2,0:T(8,128)(2,1)} copy(bf16[8,8,128,512]{3,2,1,0:T(8,128)(2,1)} %bitcast.38) | data formatting | bytes 16777216
  21.7 0.0 copy-done
  21.7 0.1 broadcast_add_fusion
  21.7 12.5 %all-gather.5.cloned.1.call-done = bf16[2,512,1024]{2,1,0:T(8,128)(2,1)} async-done(((bf16[2,128,1024]{2,1,0:T(8,128)(2,1)}), bf16[2,512,1024]{2,1,0:T(8,128)(2,1)}) %all-gather.5.cloned.1.call-update) | async-done | bytes 2097168 | tf_op jit(solution)/shard_map/all_gather | solution.py:49
  34.2 75.0 %all-gather.3.cloned.1.call-done = bf16[16,128,1024]{2,1,0:T(8,128)(2,1)} async-done(((bf16[2,128,1024]{2,1,0:T(8,128)(2,1)}), bf16[16,128,1024]{2,1,0:T(8,128)(2,1)}) %all-gather.3.cloned.1.call-update) | async-done | bytes 4194320 | tf_op jit(solution)/shard_map/all_gather | solution.py:47
  109.2 6.2 %convolution_convert_fusion.1 = bf16[2048,512]{1,0:T(8,128)(2,1)} fusion(bf16[2048,1024]{1,0:T(8,128)(2,1)} %bitcast.42, bf16[2,512,1024]{2,1,0:T(8,128)(2,1)} %all-gather.5.cloned.1.call-done), kind=kOutput, calls=%fused_computation.1 | convolution fusion | flops 2148532224 | bytes 7340032 | tf_op jit(solution)/shard_map/dot_general | solution.py:18
  115.4 2.2 %reshape.63 = bf16[16,65536]{1,0:T(8,128)(2,1)S(1)} reshape(bf16[2048,512]{1,0:T(8,128)(2,1)} %convolution_convert_fusion.1) | data formatting | bytes 4194304 | tf_op jit(solution)/shard_map/reshape | solution.py:24
  117.6 6.2 %convolution_convert_fusion = bf16[2048,512]{1,0:T(8,128)(2,1)} fusion(bf16[2048,1024]{1,0:T(8,128)(2,1)} %bitcast.43, bf16[2,512,1024]{2,1,0:T(8,128)(2,1)} %all-gather.5.cloned.1.call-done), kind=kOutput, calls=%fused_computation | convolution fusion | flops 2148532224 | bytes 7340032 | tf_op jit(solution)/shard_map/dot_general | solution.py:18
  123.8 3.2 %reshape.65 = bf16[16,65536]{1,0:T(8,128)(2,1)} reshape(bf16[2048,512]{1,0:T(8,128)(2,1)} %convolution_convert_fusion) | data formatting | bytes 4194304 | tf_op jit(solution)/shard_map/reshape | solution.py:24
  126.9 6.3 %convolution_bitcast_fusion = f32[1,16,64]{2,1,0:T(8,128)S(1)} fusion(bf16[16,65536]{1,0:T(8,128)(2,1)} %reshape.65, bf16[64,65536]{1,0:T(8,128)(2,1)} %bitcast.36), kind=kOutput, calls=%fused_computation.3 | convolution fusion | flops 134217728 | bytes 10489856 | tf_op jit(solution)/shard_map/dot_general | solution.py:26
  133.2 0.0 copy-start.1
  133.2 5.7 %convolution_bitcast_fusion.1 = f32[1,16,64]{2,1,0:T(8,128)S(1)} fusion(bf16[16,65536]{1,0:T(8,128)(2,1)S(1)} %reshape.63, bf16[64,65536]{1,0:T(8,128)(2,1)} %bitcast.37), kind=kOutput, calls=%fused_computation.4 | convolution fusion | flops 134217728 | bytes 10489856 | tf_op jit(solution)/shard_map/dot_general | solution.py:26
  138.9 0.7 reshape.71
  139.6 3.3 %all-to-all-start = ((f32[8,1,256]{2,1,0:T(1,128)}), f32[8,1,256]{2,1,0:T(1,128)S(1)}, u32[]{:S(2)}, u32[]{:S(2)}) async-start(f32[8,1,256]{2,1,0:T(1,128)} %reshape.71), calls=%async_computation | async-start | bytes 16384 | tf_op jit(solution)/shard_map/all_to_all | solution.py:51
  143.0 0.1 select_reduce_fusion.1
  143.0 0.0 copy-done.1
  143.0 0.6 dynamic-slice
  144.3 5.1 %all-to-all-done = f32[8,1,256]{2,1,0:T(1,128)S(1)} async-done(((f32[8,1,256]{2,1,0:T(1,128)}), f32[8,1,256]{2,1,0:T(1,128)S(1)}, u32[]{:S(2)}, u32[]{:S(2)}) %all-to-all-start) | async-done | bytes 8224 | tf_op jit(solution)/shard_map/all_to_all | solution.py:51
  149.4 0.5 broadcast.57
  149.9 0.7 reduce
  150.6 0.1 reshape.72
  150.7 0.2 convolution_add_fusion
  150.9 10.1 %all-reduce = f32[2,16,64]{2,1,0:T(8,128)S(1)} all-reduce(f32[2,16,64]{2,1,0:T(8,128)S(1)} %convolution_add_fusion), channel_id=2, replica_groups=mesh['ba'=8,'dev'=4] {'dev'}, use_global_device_ids=true, to_apply=%region_0.1.clone | all-reduce | flops 2048 | bytes 16384
  161.0 0.1 dynamic-slice_divide_fusion
  161.1 0.7 reshape.66
  (6 shorter events, 0.1 us)
Async XLA Ops:
  6.5 27.7 %all-gather.5.cloned.1.call-start = ((), (), s32[]{:S(2)}) async-start(), calls=%async_computation.2 | async-start | bytes 2621440 | tf_op jit(solution)/shard_map/all_gather | solution.py:49
  7.3 101.9 %all-gather.3.cloned.1.call-start = ((), (), s32[]{:S(2)}) async-start(), calls=%async_computation.1 | async-start | bytes 4718592 | tf_op jit(solution)/shard_map/all_gather | solution.py:47
  9.9 11.8 %copy-start = (s32[64]{0:T(128)S(1)}, s32[64]{0:T(128)}, u32[]{:S(2)}) copy-start(s32[64]{0:T(128)} %param.8) | copy-start | bytes 772
  133.2 9.8 %copy-start.1 = (u32[32]{0:T(128)S(1)}, u32[32]{0:T(128)}, u32[]{:S(2)}) copy-start(u32[32]{0:T(128)} %constant.57) | copy-start | bytes 388
  139.6 9.8 %all-to-all-start = ((f32[8,1,256]{2,1,0:T(1,128)}), f32[8,1,256]{2,1,0:T(1,128)S(1)}, u32[]{:S(2)}, u32[]{:S(2)}) async-start(f32[8,1,256]{2,1,0:T(1,128)} %reshape.71), calls=%async_computation | async-start | bytes 16384 | tf_op jit(solution)/shard_map/all_to_all | solution.py:51
Sparse Core Ops, SparseCore 0:
  8.9 25.2 all-gather.4
  36.3 72.7 all-gather.2
where the time goes:
time: 169 us
  waiting for transfers between devices  93.9 us (56%)
  matrix products  24.5 us (14%)
  local copies, waits for them, and re-layouts  19.8 us (12%)
  between operations  14.1 us (8%)
  blocking collectives  10.1 us (6%)
  starting transfers between devices  3.37 us (2%)
  other arithmetic  2.64 us (2%)
    all_gather x1, waiting for transfers between devices, per_device(): left_side = lax.all_gather(factors, 'ba', axis=0, tiled=True)  75 us
    unnamed x8, local copies, waits for them, and re-layouts  13.1 us
    all_gather x1, waiting for transfers between devices, per_device(): lax.all_gather(factors, 'dev', axis=1, tiled=True)  12.5 us
    dot_general x2, matrix products, integral_block(): lax.dot_general(flat_left, right_side[position], (((1,), (1,)), ((), ()))...  12.4 us
    dot_general x2, matrix products, integral_block(): lax.dot_general(integrals, flat_amps, (((1,), (1,)), ((), ())), preferred...  11.9 us
    unnamed x1, blocking collectives  10.1 us
    reshape x2, local copies, waits for them, and re-layouts, integral_block(): integrals = integrals.astype(jnp.bfloat16).reshape(left_count, -1)  5.37 us
    all_to_all x1, waiting for transfers between devices, per_device(): lax.all_to_all(ladder, 'ba', split_axis=1, concat_axis=0, tiled=True)  5.12 us
  transfers between devices with their start and end apart: 3, of which 3 were waited for; matrix products, arithmetic and copies ran while one was open for 9% of the time, Pallas kernels for 0%

commit v1 on v0

v1 whole, which is shorter than its diff:
```python
import functools

import jax
import jax.numpy as jnp
from jax import lax
from jax.experimental import pallas as pl
from jax.experimental.pallas import tpu as pltpu
from jax.sharding import PartitionSpec as P

NOCC = 8
LANES = 128
MESH = pl.DeviceIdType.MESH

level_shift = 0.3


def flip_bits(index, bits):
    result = index
    bit = 1
    while bit <= bits:
        if bits & bit:
            result = result + bit - 2 * bit * ((result // bit) % 2)
        bit *= 2
    return result


def to_column(row):
    n = row.shape[1]
    rows = lax.broadcasted_iota(jnp.int32, (n, n), 0)
    lanes = lax.broadcasted_iota(jnp.int32, (n, n), 1)
    return jnp.sum(jnp.where(rows == lanes, row, jnp.zeros_like(row)), axis=1, keepdims=True)


def kernel(
    dims,
    f_hbm,
    amps_hbm,
    order_ref,
    occ_ref,
    vir_ref,
    levels_ref,
    out_ref,
    local,
    right,
    other,
    left_f32,
    left,
    raw,
    stage,
    amps,
    ints,
    acc,
    tiles,
    parts,
    load_sem,
    own_sem,
    amp_sem,
    send_z,
    send_o,
    send_c,
    send_y,
    recv_piece,
    recv_y,
    send_f,
    recv_f,
):
    nz, ny, no, owned, cols, qs, window, pairs, virt, tile_c, amp_c = dims
    nd = no * 2
    nb = nz * owned
    total = nz * ny * nd
    split = window // nd
    ba, dev = lax.axis_index("ba"), lax.axis_index("dev")
    me = ba * nd + dev
    z, y = ba // ny, ba % ny
    outer, core = dev // 2, dev % 2
    partner_core = outer * 2 + 1 - core
    chunks = cols // amp_c

    load = pltpu.make_async_copy(f_hbm, local, load_sem)
    load.start()
    own = pltpu.make_async_copy(
        f_hbm.at[:, :, pl.ds(pl.multiple_of(z * qs, LANES), qs)], right.at[z, :, dev], own_sem
    )
    own.start()

    def amp_load(chunk):
        return pltpu.make_async_copy(
            amps_hbm.at[:, pl.ds(chunk * amp_c, amp_c), :], raw.at[chunk], amp_sem.at[chunk]
        )

    for chunk in range(chunks):
        amp_load(chunk).start()

    barrier = pltpu.get_barrier_semaphore()

    def greet(step, carry):
        there = (me + step) % total
        pl.semaphore_signal(
            barrier, inc=1, device_id=(there // nd, there % nd), device_id_type=MESH
        )
        return carry

    lax.fori_loop(1, total, greet, 0)
    load.wait()
    own.wait()
    pl.semaphore_wait(barrier, total - 1)

    def piece_copy(piece_z, piece_d, send, ba_to, dev_to):
        return pltpu.make_async_remote_copy(
            src_ref=right.at[piece_z, :, piece_d],
            dst_ref=right.at[piece_z, :, piece_d],
            send_sem=send,
            recv_sem=recv_piece.at[piece_z, piece_d],
            device_id=(ba_to, dev_to),
            device_id_type=MESH,
        )

    pending = []
    for step in range(1, nz):
        there = flip_bits(z, step)
        copy = pltpu.make_async_remote_copy(
            src_ref=local.at[:, :, pl.ds(pl.multiple_of(there * qs, LANES), qs)],
            dst_ref=right.at[z, :, dev],
            send_sem=send_z.at[step],
            recv_sem=recv_piece.at[z, dev],
            device_id=(there * ny + y, dev),
            device_id_type=MESH,
        )
        copy.start()
        pending.append(copy)

    def forward(step):
        from_z = flip_bits(z, step)
        if step:
            piece_copy(from_z, dev, send_z.at[0], ba, partner_core).wait_recv()
        for other_outer in range(1, no):
            copy = piece_copy(
                from_z,
                dev,
                send_o.at[step, other_outer],
                ba,
                flip_bits(outer, other_outer) * 2 + core,
            )
            copy.start()
            pending.append(copy)
        for other_y in range(1, ny):
            copy = pltpu.make_async_remote_copy(
                src_ref=right.at[from_z, :, dev],
                dst_ref=other.at[y, from_z],
                send_sem=send_y.at[step, other_y],
                recv_sem=recv_y.at[y, from_z],
                device_id=(z * ny + flip_bits(y, other_y), dev),
                device_id_type=MESH,
            )
            copy.start()
            pending.append(copy)
        copy = piece_copy(from_z, dev, send_c.at[step, 0], ba, partner_core)
        copy.start()
        pending.append(copy)

    def widen(source, at_y, at_z):
        for i in range(owned):
            row = (at_z * ny + at_y) * owned + i
            base = pl.multiple_of(row * (cols + 8), 8)
            for h in range(qs // LANES):
                left_f32[h, pl.ds(base, cols), :] = source[
                    i, :, h * LANES : (h + 1) * LANES
                ].astype(jnp.float32)

    def amp_chunk(chunk):
        amp_load(chunk).wait()
        pitch = amp_c + 8

        def spread(k, carry):
            base = pl.multiple_of(k * pitch, 8)
            for h in range(virt // LANES):
                stage[h, pl.ds(base, amp_c), :] = raw[
                    chunk, k, :, h * LANES : (h + 1) * LANES
                ].astype(jnp.float32)
            return carry

        lax.fori_loop(0, pairs, spread, 0, unroll=4)

        def gather(c, carry):
            for h in range(virt // LANES):
                amps[chunk * amp_c + c, :, h * LANES : (h + 1) * LANES] = stage[
                    h, pl.ds(c, pairs, stride=pitch), :
                ].astype(jnp.bfloat16)
            return carry

        lax.fori_loop(0, amp_c, gather, 0)

    done = 0
    for step in range(nz):
        forward(step)
        upto = (step + 1) * chunks // nz
        for chunk in range(done, upto):
            amp_chunk(chunk)
        done = upto
        from_z = flip_bits(z, step)
        widen(right.at[from_z, :, dev], y, from_z)

    for step in range(nz):
        from_z = flip_bits(z, step)
        for other_outer in range(1, no):
            from_d = flip_bits(outer, other_outer) * 2 + core
            piece_copy(from_z, from_d, send_z.at[0], ba, partner_core).wait_recv()
            copy = piece_copy(from_z, from_d, send_c.at[step, other_outer], ba, partner_core)
            copy.start()
            pending.append(copy)
        for other_y in range(1, ny):
            from_y = flip_bits(y, other_y)
            pltpu.make_async_remote_copy(
                src_ref=right.at[from_z, :, dev],
                dst_ref=other.at[from_y, from_z],
                send_sem=send_z.at[0],
                recv_sem=recv_y.at[from_y, from_z],
                device_id=(ba, partner_core),
                device_id_type=MESH,
            ).wait_recv()
            widen(other.at[from_y, from_z], from_y, from_z)

    def turn(c, carry):
        rows = pl.ds(pl.multiple_of(c * window, window), window)
        for h in range(qs // LANES):
            left[rows, h * LANES : (h + 1) * LANES] = left_f32[
                h, pl.ds(c, window, stride=cols + 8), :
            ].astype(jnp.bfloat16)
        return carry

    lax.fori_loop(0, cols, turn, 0, unroll=4)

    for step in range(nz):
        from_z = flip_bits(z, step)
        for other_outer in range(no):
            from_d = flip_bits(outer, other_outer) * 2 + 1 - core
            piece_copy(from_z, from_d, send_z.at[0], ba, partner_core).wait_recv()

    acc[...] = jnp.zeros_like(acc)
    block = tile_c * window

    def contract(ct, carry):
        rows = left[pl.ds(pl.multiple_of(ct * block, block), block), :]
        for b in range(nb):
            side = right[b // owned, b % owned].reshape(virt, qs)
            part = lax.dot_general(
                rows, side, (((1,), (1,)), ((), ())), preferred_element_type=jnp.float32
            )
            ints[:, b * window : (b + 1) * window, :] = part.astype(jnp.bfloat16).reshape(
                tile_c, window, virt
            )

        def add(t, value):
            return value + lax.dot_general(
                ints[t],
                amps[ct * tile_c + t],
                (((1,), (1,)), ((), ())),
                preferred_element_type=jnp.float32,
            )

        acc[:, :, 0:pairs] += lax.fori_loop(
            0, tile_c, add, jnp.zeros((nb * window, pairs), jnp.float32), unroll=4
        ).reshape(nb, window, pairs)
        return carry

    lax.fori_loop(0, cols // tile_c, contract, 0)
    acc[:, :, pairs : 2 * pairs] = acc[:, :, 0:pairs]

    height = owned * split
    row_at = lax.broadcasted_iota(jnp.int32, (height, 2 * pairs), 0)
    lane_at = lax.broadcasted_iota(jnp.int32, (height, 2 * pairs), 1)

    def make_tile(there):
        to_ba, to_dev = there // nd, there % nd
        to_z, to_y = to_ba // ny, to_ba % ny
        straight = jnp.zeros((height, 2 * pairs), jnp.float32)
        pieces = []
        turned = []
        for i in range(owned):
            pieces.append(acc[to_z * owned + i, pl.ds(to_dev * split, split), :])
            for a in range(split):
                row = to_dev * split + a
                owner = row // owned
                turned.append(
                    acc[(owner // ny) * owned + row % owned, pl.ds(to_ba * owned + i, 1), :]
                )
        straight = jnp.concatenate(pieces, axis=0)
        flipped = jnp.concatenate(turned, axis=0)
        same = jnp.zeros((height, 2 * pairs), jnp.int32) + to_y == y
        owner_at = (to_dev * split + row_at % split) // owned
        return jnp.where(
            lane_at < pairs,
            jnp.where(same, straight, 0.0),
            jnp.where(owner_at % ny == y, flipped, 0.0),
        )

    def tile_copy(there):
        return pltpu.make_async_remote_copy(
            src_ref=tiles.at[there],
            dst_ref=parts.at[me],
            send_sem=send_f.at[there],
            recv_sem=recv_f.at[me],
            device_id=(there // nd, there % nd),
            device_id_type=MESH,
        )

    def send_tile(step, carry):
        there = (me + step) % total
        tiles[there] = make_tile(there)
        tile_copy(there).start()
        return carry

    lax.fori_loop(1, total, send_tile, 0)
    parts[me] = make_tile(me)

    levels = to_column(levels_ref[...])
    level_at = lax.broadcasted_iota(jnp.int32, (levels.shape[0], window), 0)
    virtual = jnp.sum(
        jnp.where(level_at == vir_ref[...], levels, 0.0), axis=0, keepdims=True
    )
    level_occ = lax.broadcasted_iota(jnp.int32, (levels.shape[0], NOCC), 0)
    occupied = to_column(
        -jnp.sum(jnp.where(level_occ == occ_ref[...], levels, 0.0), axis=0, keepdims=True)
    )
    order = order_ref[...]
    first, second = order // NOCC, order % NOCC
    occ_at = lax.broadcasted_iota(jnp.int32, (NOCC, pairs), 0)
    pair_energy = jnp.sum(
        jnp.where(occ_at == first, occupied, 0.0), axis=0, keepdims=True
    ) + jnp.sum(jnp.where(occ_at == second, occupied, 0.0), axis=0, keepdims=True)
    win_row = lax.broadcasted_iota(jnp.int32, (height, window), 0)
    win_lane = lax.broadcasted_iota(jnp.int32, (height, window), 1)
    right_energy = jnp.sum(
        jnp.where(win_lane == ba * owned + win_row // split, virtual, 0.0), axis=1, keepdims=True
    )
    left_energy = jnp.sum(
        jnp.where(win_lane == dev * split + win_row % split, virtual, 0.0), axis=1, keepdims=True
    )
    denominator = right_energy + left_energy - pair_energy + level_shift
    permuter = (to_column(order) == second * NOCC + first).astype(jnp.float32)

    def arrive(step, carry):
        there = (me + step) % total
        pltpu.make_async_remote_copy(
            src_ref=tiles.at[there],
            dst_ref=parts.at[there],
            send_sem=send_f.at[there],
            recv_sem=recv_f.at[there],
            device_id=(there // nd, there % nd),
            device_id_type=MESH,
        ).wait_recv()
        return carry

    lax.fori_loop(1, total, arrive, 0)
    summed = jnp.sum(parts[...], axis=0)
    moved = jnp.dot(
        summed[:, pairs:],
        permuter,
        precision=lax.Precision.HIGHEST,
        preferred_element_type=jnp.float32,
    )
    result = (summed[:, :pairs] + moved) / denominator
    for i in range(owned):
        for a in range(split):
            out_ref[i : i + 1, a * pairs : (a + 1) * pairs] = result[
                i * split + a : i * split + a + 1, :
            ]

    for copy in pending:
        copy.wait_send()

    def sent(step, carry):
        tile_copy((me + step) % total).wait_send()
        return carry

    lax.fori_loop(1, total, sent, 0)


def per_device(nba, ndev, factors, amplitudes, pair_order, occ_bin, vir_bin, levels):
    owned, cols, fitting = factors.shape
    pairs, _, virt = amplitudes.shape
    window = owned * nba
    ny = 1
    while ny * ny * 4 <= nba:
        ny *= 2
    nz = nba // ny
    no = ndev // 2
    qs = fitting // nz
    nb = nz * owned
    split = window // ndev
    total = nba * ndev
    tile_c = min(cols, max(1, (4 << 20) // (nb * window * virt * 2)))
    amp_c = 16
    dims = (nz, ny, no, owned, cols, qs, window, pairs, virt, tile_c, amp_c)
    dma = pltpu.SemaphoreType.DMA
    vmem = pl.BlockSpec(memory_space=pltpu.VMEM)
    hbm = pl.BlockSpec(memory_space=pl.ANY)
    return pl.pallas_call(
        functools.partial(kernel, dims),
        out_shape=jax.ShapeDtypeStruct((owned, split * pairs), jnp.float32),
        in_specs=[hbm, hbm, vmem, vmem, vmem, vmem],
        out_specs=vmem,
        scratch_shapes=[
            pltpu.VMEM((owned, cols, fitting), jnp.bfloat16),
            pltpu.VMEM((nz, owned, ndev, cols, qs), jnp.bfloat16),
            pltpu.VMEM((ny, nz, owned, cols, qs), jnp.bfloat16),
            pltpu.VMEM((qs // LANES, window * (cols + 8), LANES), jnp.float32),
            pltpu.VMEM((cols * window, qs), jnp.bfloat16),
            pltpu.VMEM((cols // amp_c, pairs, amp_c, virt), jnp.bfloat16),
            pltpu.VMEM((virt // LANES, pairs * (amp_c + 8), LANES), jnp.float32),
            pltpu.VMEM((cols, pairs, virt), jnp.bfloat16),
            pltpu.VMEM((tile_c, nb * window, virt), jnp.bfloat16),
            pltpu.VMEM((nb, window, 2 * pairs), jnp.float32),
            pltpu.VMEM((total, owned * split, 2 * pairs), jnp.float32),
            pltpu.VMEM((total, owned * split, 2 * pairs), jnp.float32),
            dma,
            dma,
            dma((cols // amp_c,)),
            dma((nz,)),
            dma((nz, no)),
            dma((nz, no)),
            dma((nz, ny)),
            dma((nz, ndev)),
            dma((ny, nz)),
            dma((total,)),
            dma((total,)),
        ],
        compiler_params=pltpu.CompilerParams(
            collective_id=0, has_side_effects=True, vmem_limit_bytes=56 << 20
        ),
    )(
        factors,
        amplitudes,
        pair_order.reshape(1, -1),
        occ_bin.reshape(1, -1),
        vir_bin.reshape(1, -1),
        levels.reshape(1, -1),
    )


def solution(mesh):
    return jax.shard_map(
        functools.partial(per_device, mesh.shape["ba"], mesh.shape["dev"]),
        mesh=mesh,
        in_specs=(P("ba", "dev", None), P(None, "dev", None), P(), P(), P(), P()),
        out_specs=P("ba", "dev"),
        check_vma=False,
    )
```

time: 169 us -> 49 us (0.29)
  waiting for transfers between devices: 93.9 us -> 0 us
  Pallas kernels: 0 us -> 47.6 us
  matrix products: 24.5 us -> 0 us
  local copies, waits for them, and re-layouts: 19.8 us -> 1.26 us
  between operations: 14.1 us -> 0.01 us
  blocking collectives: 10.1 us -> 0 us
  starting transfers between devices: 3.37 us -> 0 us
  other arithmetic: 2.64 us -> 0 us
    all_gather x2 -> x0, waiting for transfers between devices: 87.4 us -> none  [the longest x1 75 us: per_device(): left_side = lax.all_gather(factors, 'ba', axis=0, tiled=True)]
    pallas_call x0 -> x1, Pallas kernels: none -> 47.6 us  [per_device(): pl.pallas_call(functools.partial(kernel, dims), out_shape=jax.ShapeDtypeS...]
    dot_general x5 -> x0, matrix products: 24.5 us -> none  [the longest x2 12.4 us: integral_block(): lax.dot_general(flat_left, right_side[position], (((1,), (1,)), ((), ()))...]
    unnamed x8 -> x1, local copies, waits for them, and re-layouts: 13.1 us -> 1.26 us
    unnamed x1 -> x0, blocking collectives: 10.1 us -> none
    reshape x3 -> x0, local copies, waits for them, and re-layouts: 6.03 us -> none  [the longest x2 5.37 us: integral_block(): integrals = integrals.astype(jnp.bfloat16).reshape(left_count, -1)]
    all_to_all x1 -> x0, waiting for transfers between devices: 5.12 us -> none  [per_device(): lax.all_to_all(ladder, 'ba', split_axis=1, concat_axis=0, tiled=True)]
    all_to_all x1 -> x0, starting transfers between devices: 3.33 us -> none  [per_device(): lax.all_to_all(ladder, 'ba', split_axis=1, concat_axis=0, tiled=True)]
  transfers between devices with their start and end apart: 3 -> 0, of which waited for: 3 -> 0; matrix products, arithmetic and copies ran while one was open for 9% -> 0% of each run, Pallas kernels for 0% -> 0%
where the time goes in v1:
time: 49 us; the launch traced here: 48.8 us
  Pallas kernels  47.6 us (97%)
  local copies, waits for them, and re-layouts  1.26 us (3%)
    pallas_call x1, Pallas kernels, per_device(): pl.pallas_call(functools.partial(kernel, dims), out_shape=jax.ShapeDtypeS...  47.6 us
    unnamed x1, local copies, waits for them, and re-layouts  1.26 us

profile of v1, /device:TPU:0, one launch (start us, length us, event | category | flops | bytes accessed | tf_op | source)
XLA Modules:
  0.0 48.8 jit_solution(4668024827955493001)
XLA Ops:
  0.0 47.6 %shard_map.64 = f32[2,256]{1,0:T(2,128)} custom-call(bf16[2,128,1024]{2,1,0:T(8,128)(2,1)} %f_hbm.1, bf16[64,128,512]{2,1,0:T(8,128)(2,1)} %amps_hbm.1, s32[1,64]{1,0:T(1,128)} %bitcast.4, s32[1,8]{1,0:T(1,128)} %bitcast.5, s32[1,16]{1,0:T(1,128)} %bitcast.6, f32[1,128]{1,0:T(1,128)} %bitcast.7), custom_call_target="tpu_custom_call" | custom-call | tf_op jit(solution)/shard_map/pallas_call | solution.py:398
  47.6 1.3 %copy.8 = f32[2,256]{1,0:T(2,128)} copy(f32[2,256]{1,0:T(2,128)} %shard_map.64) | data formatting | bytes 4096

commit v2 on v1

--- a/solution.py
+++ b/solution.py
@@ -49,6 +49,7 @@
     stage,
     amps,
     ints,
+    flat,
     acc,
     tiles,
     parts,
@@ -75,6 +76,9 @@
     outer, core = dev // 2, dev % 2
     partner_core = outer * 2 + 1 - core
     chunks = cols // amp_c
+    half, half_z = window // 2, nz // 2
+    mine = z // half_z
+    halves = (mine, 1 - mine)
 
     load = pltpu.make_async_copy(f_hbm, local, load_sem)
     load.start()
@@ -105,39 +109,44 @@
     own.wait()
     pl.semaphore_wait(barrier, total - 1)
 
-    def piece_copy(piece_z, piece_d, send, ba_to, dev_to):
+    def piece_copy(piece_z, row, piece_d, send, ba_to, dev_to):
         return pltpu.make_async_remote_copy(
-            src_ref=right.at[piece_z, :, piece_d],
-            dst_ref=right.at[piece_z, :, piece_d],
+            src_ref=right.at[piece_z, row, piece_d],
+            dst_ref=right.at[piece_z, row, piece_d],
             send_sem=send,
-            recv_sem=recv_piece.at[piece_z, piece_d],
+            recv_sem=recv_piece.at[piece_z, row, piece_d],
             device_id=(ba_to, dev_to),
             device_id_type=MESH,
         )
 
+    def await_piece(piece_z, row, piece_d):
+        piece_copy(piece_z, row, piece_d, send_z.at[0, 0], ba, partner_core).wait_recv()
+
     pending = []
     for step in range(1, nz):
         there = flip_bits(z, step)
-        copy = pltpu.make_async_remote_copy(
-            src_ref=local.at[:, :, pl.ds(pl.multiple_of(there * qs, LANES), qs)],
-            dst_ref=right.at[z, :, dev],
-            send_sem=send_z.at[step],
-            recv_sem=recv_piece.at[z, dev],
-            device_id=(there * ny + y, dev),
-            device_id_type=MESH,
-        )
-        copy.start()
-        pending.append(copy)
-
-    def forward(step):
+        for row in range(owned):
+            copy = pltpu.make_async_remote_copy(
+                src_ref=local.at[row, :, pl.ds(pl.multiple_of(there * qs, LANES), qs)],
+                dst_ref=right.at[z, row, dev],
+                send_sem=send_z.at[step, row],
+                recv_sem=recv_piece.at[z, row, dev],
+                device_id=(there * ny + y, dev),
+                device_id_type=MESH,
+            )
+            copy.start()
+            pending.append(copy)
+
+    def forward(step, row):
         from_z = flip_bits(z, step)
         if step:
-            piece_copy(from_z, dev, send_z.at[0], ba, partner_core).wait_recv()
+            await_piece(from_z, row, dev)
         for other_outer in range(1, no):
             copy = piece_copy(
                 from_z,
+                row,
                 dev,
-                send_o.at[step, other_outer],
+                send_o.at[step, row, other_outer],
                 ba,
                 flip_bits(outer, other_outer) * 2 + core,
             )
@@ -145,16 +154,16 @@
             pending.append(copy)
         for other_y in range(1, ny):
             copy = pltpu.make_async_remote_copy(
-                src_ref=right.at[from_z, :, dev],
-                dst_ref=other.at[y, from_z],
-                send_sem=send_y.at[step, other_y],
-                recv_sem=recv_y.at[y, from_z],
+                src_ref=right.at[from_z, row, dev],
+                dst_ref=other.at[y, from_z, row],
+                send_sem=send_y.at[step, row, other_y],
+                recv_sem=recv_y.at[y, from_z, row],
                 device_id=(z * ny + flip_bits(y, other_y), dev),
                 device_id_type=MESH,
             )
             copy.start()
             pending.append(copy)
-        copy = piece_copy(from_z, dev, send_c.at[step, 0], ba, partner_core)
+        copy = piece_copy(from_z, row, dev, send_c.at[step, row, 0], ba, partner_core)
         copy.start()
         pending.append(copy)
 
@@ -190,80 +199,143 @@
 
         lax.fori_loop(0, amp_c, gather, 0)
 
-    done = 0
-    for step in range(nz):
-        forward(step)
-        upto = (step + 1) * chunks // nz
-        for chunk in range(done, upto):
-            amp_chunk(chunk)
-        done = upto
+    def own_rows(step):
         from_z = flip_bits(z, step)
         widen(right.at[from_z, :, dev], y, from_z)
 
-    for step in range(nz):
+    def collect(step):
         from_z = flip_bits(z, step)
-        for other_outer in range(1, no):
-            from_d = flip_bits(outer, other_outer) * 2 + core
-            piece_copy(from_z, from_d, send_z.at[0], ba, partner_core).wait_recv()
-            copy = piece_copy(from_z, from_d, send_c.at[step, other_outer], ba, partner_core)
-            copy.start()
-            pending.append(copy)
+        for row in range(owned):
+            for other_outer in range(1, no):
+                from_d = flip_bits(outer, other_outer) * 2 + core
+                await_piece(from_z, row, from_d)
+                copy = piece_copy(
+                    from_z, row, from_d, send_c.at[step, row, other_outer], ba, partner_core
+                )
+                copy.start()
+                pending.append(copy)
         for other_y in range(1, ny):
             from_y = flip_bits(y, other_y)
-            pltpu.make_async_remote_copy(
-                src_ref=right.at[from_z, :, dev],
-                dst_ref=other.at[from_y, from_z],
-                send_sem=send_z.at[0],
-                recv_sem=recv_y.at[from_y, from_z],
-                device_id=(ba, partner_core),
-                device_id_type=MESH,
-            ).wait_recv()
+            for row in range(owned):
+                pltpu.make_async_remote_copy(
+                    src_ref=right.at[from_z, row, dev],
+                    dst_ref=other.at[from_y, from_z, row],
+                    send_sem=send_z.at[0, 0],
+                    recv_sem=recv_y.at[from_y, from_z, row],
+                    device_id=(ba, partner_core),
+                    device_id_type=MESH,
+                ).wait_recv()
             widen(other.at[from_y, from_z], from_y, from_z)
 
-    def turn(c, carry):
-        rows = pl.ds(pl.multiple_of(c * window, window), window)
-        for h in range(qs // LANES):
-            left[rows, h * LANES : (h + 1) * LANES] = left_f32[
-                h, pl.ds(c, window, stride=cols + 8), :
-            ].astype(jnp.bfloat16)
-        return carry
-
-    lax.fori_loop(0, cols, turn, 0, unroll=4)
-
-    for step in range(nz):
+    def finish(step):
         from_z = flip_bits(z, step)
-        for other_outer in range(no):
-            from_d = flip_bits(outer, other_outer) * 2 + 1 - core
-            piece_copy(from_z, from_d, send_z.at[0], ba, partner_core).wait_recv()
-
-    acc[...] = jnp.zeros_like(acc)
-    block = tile_c * window
-
-    def contract(ct, carry):
-        rows = left[pl.ds(pl.multiple_of(ct * block, block), block), :]
-        for b in range(nb):
-            side = right[b // owned, b % owned].reshape(virt, qs)
-            part = lax.dot_general(
-                rows, side, (((1,), (1,)), ((), ())), preferred_element_type=jnp.float32
-            )
-            ints[:, b * window : (b + 1) * window, :] = part.astype(jnp.bfloat16).reshape(
-                tile_c, window, virt
-            )
+        for row in range(owned):
+            for other_outer in range(no):
+                await_piece(from_z, row, flip_bits(outer, other_outer) * 2 + 1 - core)
+
+    def turn_half(side):
+        first_row = halves[side] * half * (cols + 8)
+
+        def turn(step, carry):
+            at = step * 2
+            rows = pl.ds(pl.multiple_of(at * half, 2 * half), 2 * half)
+            for h in range(qs // LANES):
+                left[side, rows, h * LANES : (h + 1) * LANES] = jnp.concatenate(
+                    [
+                        left_f32[h, pl.ds(first_row + at + i, half, stride=cols + 8), :]
+                        for i in range(2)
+                    ],
+                    axis=0,
+                ).astype(jnp.bfloat16)
+            return carry
+
+        lax.fori_loop(0, cols // 2, turn, 0, unroll=4)
+
+    block = tile_c * half
+    early = [(0, 0, j) for j in range(half_z)]
+    late = [(1, side, j) for side in range(2) for j in range(half_z)] + [
+        (0, 1, j) for j in range(half_z)
+    ]
+    height_of = owned * half
+
+    def contract(ct, jobs, base):
+        for at, (a_side, b_side, j) in enumerate(jobs):
+            rows = left[a_side, pl.ds(pl.multiple_of(ct * block, block), block), :]
+            from_z = halves[b_side] * half_z + j
+            parts_of = []
+            for i in range(owned):
+                side = right[from_z, i].reshape(virt, qs)
+                parts_of.append(
+                    lax.dot_general(
+                        rows, side, (((1,), (1,)), ((), ())), preferred_element_type=jnp.float32
+                    ).reshape(tile_c, half, virt)
+                )
+            ints[:, at * height_of : (at + 1) * height_of, :] = jnp.concatenate(
+                parts_of, axis=1
+            ).astype(jnp.bfloat16)
+        count = len(jobs) * height_of
 
         def add(t, value):
             return value + lax.dot_general(
-                ints[t],
+                ints[t, 0:count, :],
                 amps[ct * tile_c + t],
                 (((1,), (1,)), ((), ())),
                 preferred_element_type=jnp.float32,
             )
 
-        acc[:, :, 0:pairs] += lax.fori_loop(
-            0, tile_c, add, jnp.zeros((nb * window, pairs), jnp.float32), unroll=4
-        ).reshape(nb, window, pairs)
+        flat[base : base + count, :] += lax.fori_loop(
+            0, tile_c, add, jnp.zeros((count, pairs), jnp.float32), unroll=tile_c
+        )
+
+    flat[...] = jnp.zeros_like(flat)
+    done = 0
+    for step in range(half_z):
+        for row in range(owned):
+            forward(step, row)
+            upto = (step * owned + row + 1) * chunks // (half_z * owned)
+            for chunk in range(done, upto):
+                amp_chunk(chunk)
+            done = upto
+        own_rows(step)
+    for step in range(half_z, nz - 1):
+        for row in range(owned):
+            forward(step, row)
+    for step in range(half_z):
+        collect(step)
+    turn_half(0)
+    for step in range(half_z):
+        finish(step)
+    contract(0, early, 0)
+    for row in range(owned):
+        forward(nz - 1, row)
+
+    def early_tile(ct, carry):
+        contract(ct, early, 0)
         return carry
 
-    lax.fori_loop(0, cols // tile_c, contract, 0)
+    lax.fori_loop(1, cols // tile_c, early_tile, 0)
+    for step in range(half_z, nz):
+        own_rows(step)
+    for step in range(half_z, nz):
+        collect(step)
+    turn_half(1)
+    for step in range(half_z, nz):
+        finish(step)
+    late_base = len(early) * height_of
+
+    def late_tile(ct, carry):
+        contract(ct, late, late_base)
+        return carry
+
+    lax.fori_loop(0, cols // tile_c, late_tile, 0)
+    for at, (a_side, b_side, j) in enumerate(early + late):
+        for i in range(owned):
+            value = flat[at * height_of + i * half : at * height_of + (i + 1) * half, :]
+            acc[
+                (halves[b_side] * half_z + j) * owned + i,
+                pl.ds(pl.multiple_of(halves[a_side] * half, 8), half),
+                0:pairs,
+            ] = value
     acc[:, :, pairs : 2 * pairs] = acc[:, :, 0:pairs]
 
     height = owned * split
@@ -405,23 +477,24 @@
             pltpu.VMEM((nz, owned, ndev, cols, qs), jnp.bfloat16),
             pltpu.VMEM((ny, nz, owned, cols, qs), jnp.bfloat16),
             pltpu.VMEM((qs // LANES, window * (cols + 8), LANES), jnp.float32),
-            pltpu.VMEM((cols * window, qs), jnp.bfloat16),
+            pltpu.VMEM((2, cols * window // 2, qs), jnp.bfloat16),
             pltpu.VMEM((cols // amp_c, pairs, amp_c, virt), jnp.bfloat16),
             pltpu.VMEM((virt // LANES, pairs * (amp_c + 8), LANES), jnp.float32),
             pltpu.VMEM((cols, pairs, virt), jnp.bfloat16),
             pltpu.VMEM((tile_c, nb * window, virt), jnp.bfloat16),
+            pltpu.VMEM((nb * window, pairs), jnp.float32),
             pltpu.VMEM((nb, window, 2 * pairs), jnp.float32),
             pltpu.VMEM((total, owned * split, 2 * pairs), jnp.float32),
             pltpu.VMEM((total, owned * split, 2 * pairs), jnp.float32),
             dma,
             dma,
             dma((cols // amp_c,)),
-            dma((nz,)),
-            dma((nz, no)),
-            dma((nz, no)),
-            dma((nz, ny)),
-            dma((nz, ndev)),
-            dma((ny, nz)),
+            dma((nz, owned)),
+            dma((nz, owned, no)),
+            dma((nz, owned, no)),
+            dma((nz, owned, ny)),
+            dma((nz, owned, ndev)),
+            dma((ny, nz, owned)),
             dma((total,)),
             dma((total,)),
         ],

time: 49 us -> 43.6 us (0.89)
  Pallas kernels: 47.6 us -> 42.1 us
    pallas_call x1, Pallas kernels: 47.6 us -> 42.1 us  [per_device(): pl.pallas_call(functools.partial(kernel, dims), out_shape=jax.ShapeDtypeS...]
where the time goes in v2:
time: 43.6 us; the launch traced here: 43.4 us
  Pallas kernels  42.1 us (97%)
  local copies, waits for them, and re-layouts  1.26 us (3%)
    pallas_call x1, Pallas kernels, per_device(): pl.pallas_call(functools.partial(kernel, dims), out_shape=jax.ShapeDtypeS...  42.1 us
    unnamed x1, local copies, waits for them, and re-layouts  1.26 us

profile of v2, /device:TPU:0, one launch (start us, length us, event | category | flops | bytes accessed | tf_op | source)
XLA Modules:
  0.0 43.4 jit_solution(13181532726824374038)
XLA Ops:
  0.0 42.1 %shard_map.64 = f32[2,256]{1,0:T(2,128)} custom-call(bf16[2,128,1024]{2,1,0:T(8,128)(2,1)} %f_hbm.1, bf16[64,128,512]{2,1,0:T(8,128)(2,1)} %amps_hbm.1, s32[1,64]{1,0:T(1,128)} %bitcast.4, s32[1,8]{1,0:T(1,128)} %bitcast.5, s32[1,16]{1,0:T(1,128)} %bitcast.6, f32[1,128]{1,0:T(1,128)} %bitcast.7), custom_call_target="tpu_custom_call" | custom-call | tf_op jit(solution)/shard_map/pallas_call | solution.py:470
  42.1 1.3 %copy.8 = f32[2,256]{1,0:T(2,128)} copy(f32[2,256]{1,0:T(2,128)} %shard_map.64) | data formatting | bytes 4096

commit v3 on v2

--- a/solution.py
+++ b/solution.py
@@ -305,7 +305,6 @@
     turn_half(0)
     for step in range(half_z):
         finish(step)
-    contract(0, early, 0)
     for row in range(owned):
         forward(nz - 1, row)
 
@@ -313,7 +312,7 @@
         contract(ct, early, 0)
         return carry
 
-    lax.fori_loop(1, cols // tile_c, early_tile, 0)
+    lax.fori_loop(0, cols // tile_c, early_tile, 0)
     for step in range(half_z, nz):
         own_rows(step)
     for step in range(half_z, nz):

time: 43.6 us -> 42.9 us (0.984)
  Pallas kernels: 42.1 us -> 41.4 us
    pallas_call x1, Pallas kernels: 42.1 us -> 41.4 us  [per_device(): pl.pallas_call(functools.partial(kernel, dims), out_shape=jax.ShapeDtypeS...]
where the time goes in v3:
time: 42.9 us; the launch traced here: 42.7 us
  Pallas kernels  41.4 us (97%)
  local copies, waits for them, and re-layouts  1.26 us (3%)
    pallas_call x1, Pallas kernels, per_device(): pl.pallas_call(functools.partial(kernel, dims), out_shape=jax.ShapeDtypeS...  41.4 us
    unnamed x1, local copies, waits for them, and re-layouts  1.26 us

profile of v3, /device:TPU:0, one launch (start us, length us, event | category | flops | bytes accessed | tf_op | source)
XLA Modules:
  0.0 42.7 jit_solution(18365996149714648291)
XLA Ops:
  0.0 41.4 %shard_map.64 = f32[2,256]{1,0:T(2,128)} custom-call(bf16[2,128,1024]{2,1,0:T(8,128)(2,1)} %f_hbm.1, bf16[64,128,512]{2,1,0:T(8,128)(2,1)} %amps_hbm.1, s32[1,64]{1,0:T(1,128)} %bitcast.4, s32[1,8]{1,0:T(1,128)} %bitcast.5, s32[1,16]{1,0:T(1,128)} %bitcast.6, f32[1,128]{1,0:T(1,128)} %bitcast.7), custom_call_target="tpu_custom_call" | custom-call | tf_op jit(solution)/shard_map/pallas_call | solution.py:469
  41.5 1.3 %copy.8 = f32[2,256]{1,0:T(2,128)} copy(f32[2,256]{1,0:T(2,128)} %shard_map.64) | data formatting | bytes 4096
